TPU v7x, 32 devices: a whole 2x2x4 slice. The times are simulated.
32 devices in a mesh: gx: 2 (over x), gy: 4 (over z), gz: 4 (over y, core).
Axes of the slice: x: 2, y: 2, z: 4, core: 2. Of those that a mesh axis runs over, the one named last changes fastest.
Arguments:
- displacement: bfloat16 [3, 8, 128, 64], P(None, 'gx', 'gy', 'gz'), may hold values from -6 to 6
- lift_weight: bfloat16 [27, 64, 3], replicated, may hold values from -1 to 1
- encode_weight: bfloat16 [27, 64, 64], replicated, may hold values from -0.21875 to 0.21875
- downward_weight: bfloat16 [8, 128, 64], replicated, may hold values from -0.375 to 0.375
- middle_first: bfloat16 [27, 128, 128], replicated, may hold values from -0.15625 to 0.15625
- middle_second: bfloat16 [27, 128, 128], replicated, may hold values from -0.15625 to 0.15625
- up_weight: bfloat16 [8, 64, 128], replicated, may hold values from -0.75 to 0.75
- decode_weight: bfloat16 [27, 64, 128], replicated, may hold values from -0.15625 to 0.15625
- head_weight: bfloat16 [3, 64], replicated, may hold values from -1 to 1
Outputs:
- imitated: float32 [3, 8, 128, 64], P(None, 'gx', 'gy', 'gz')
All inputs are finite; a program needn't handle non-finite values.
Results may differ from a plain program's by a relative error of at most 0.0055.
Values may be sent and summed in bfloat16 or wider, within the bound.
A program may use at most 64 MiB of HBM per device.

v0:
```python
import functools

import jax
import jax.numpy as jnp
from jax import lax
from jax.experimental import pallas as pl
from jax.experimental.pallas import tpu as pltpu
from jax.sharding import PartitionSpec as P

AXES = ("gx", "gy", "gz")
MESH = pl.DeviceIdType.MESH
NT = (((1,), (1,)), ((), ()))
DIRS = [
    (dx, dy, dz) for dx in (-1, 0, 1) for dy in (-1, 0, 1) for dz in (-1, 0, 1)
    if (dx, dy, dz) != (0, 0, 0)
]
F32, BF16 = jnp.float32, jnp.bfloat16
RIM = 8


def leaky(value):
    return jnp.maximum(value, 0.1 * value)


def rounded(value):
    return leaky(value).astype(BF16)


def dot(rows, weight):
    return lax.dot_general(rows, weight, NT, preferred_element_type=F32)


def neighbour(direction):
    return tuple(
        lax.rem(lax.axis_index(axis) + lax.axis_size(axis) + step, lax.axis_size(axis))
        for axis, step in zip(AXES, direction)
    )


def exchange(body, below, above, first, last, sends, recvs, zc):
    size_x, size_y = body.shape[0] - 2, body.shape[1] - 2
    copies = []
    for number, (dx, dy, dz) in enumerate(DIRS):
        def span(step, size, offset):
            if step == 0:
                return (offset, size, 1)
            return (offset + size - 1, 1, 0) if step > 0 else (offset, 1, size + 1)

        if dz == 0:
            sx, nx, tx = span(dx, size_x, 1)
            sy, ny, ty = span(dy, size_y, 1)
            src = body.at[pl.ds(sx, nx), pl.ds(sy, ny)]
            dst = body.at[pl.ds(tx, nx), pl.ds(ty, ny)]
        else:
            sx, nx, tx = span(dx, size_x, 0)
            sy, ny, ty = span(dy, size_y, 0)
            src = (last if dz > 0 else first).at[pl.ds(sx, nx), pl.ds(sy, ny)]
            dst = (below if dz > 0 else above).at[pl.ds(tx, nx), pl.ds(ty, ny)]
        copies.append(
            pltpu.make_async_remote_copy(
                src_ref=src, dst_ref=dst, send_sem=sends.at[number], recv_sem=recvs.at[number],
                device_id=neighbour((dx, dy, dz)), device_id_type=MESH,
            )
        )
    return copies


def launch(copies):
    for copy in copies:
        copy.start()


def send_cells(block, before, after, first, last, sends, recvs):
    size_x, size_y = block.shape[0] - 4, block.shape[1] - 2
    copies = []
    for number, (dx, dy, dz) in enumerate(DIRS):
        sx, nx, tx = {0: (2, size_x, 2), 1: (size_x, 2, 0), -1: (2, 2, size_x + 2)}[dx]
        sy, ny, ty = {0: (0, size_y, 1), 1: (size_y - 1, 1, 0), -1: (0, 1, size_y + 1)}[dy]
        if dz == 0:
            src = block.at[pl.ds(sx, nx), pl.ds(sy + 1, ny)]
            dst = block.at[pl.ds(tx, nx), pl.ds(ty, ny)]
        else:
            src = (last if dz > 0 else first).at[pl.ds(sy, ny)]
            dst = (before if dz > 0 else after).at[1 - dx, pl.ds(ty, ny)]
        copies.append(
            pltpu.make_async_remote_copy(
                src_ref=src, dst_ref=dst, send_sem=sends.at[number], recv_sem=recvs.at[number],
                device_id=neighbour((dx, dy, dz)), device_id_type=MESH,
            )
        )
    for copy in copies:
        copy.start()
    return copies


def build_fine(raw, wide, lo, hi):
    out = raw.shape[1]
    blank = jnp.zeros((2 * out, wide.shape[2]), BF16)
    zero = jnp.zeros((out, hi - lo), BF16)
    for a in range(3):
        wide[4 * a, 2 * out :, :] = blank
        wide[4 * a + 3, : 2 * out, :] = blank
        for b in range(3):
            taps = [raw[9 * a + 3 * b + c][:, lo:hi] for c in range(3)]
            low = jnp.concatenate([taps[1], taps[2], zero, taps[0]], axis=1)
            high = jnp.concatenate([taps[0], taps[1], taps[2], zero], axis=1)
            pair = jnp.concatenate([low, high], axis=0)
            wide[4 * a + b, : 2 * out, :] = pair
            wide[4 * a + b + 1, 2 * out :, :] = pair


def masks(rows, zc):
    row = lax.rem(lax.broadcasted_iota(jnp.int32, (rows, 128), 0), zc)
    return row == 0, row == zc - 1


def half_mask(rows):
    return lax.broadcasted_iota(jnp.int32, (rows, 128), 1) < 64


def flat(plane):
    return plane.astype(F32).reshape(plane.shape[0] * plane.shape[1], 128)


def spread(edge, zc):
    return jnp.broadcast_to(edge, (edge.shape[0], zc, 128)).reshape(edge.shape[0] * zc, 128)


def shifted(plane, below, above, zc):
    rows = plane.shape[0]
    start, end = masks(rows, zc)
    down = jnp.where(start, below, pltpu.roll(plane, 1, 0))
    up = jnp.where(end, above, pltpu.roll(plane, rows - 1, 0))
    return down, up


def fine_conv(plane, twin, weight, x0, group, size_y, zc):
    summed = None
    pairs = size_y // 2
    for a in range(3):
        parts = []
        for source in (plane, twin):
            halves = [[], []]
            for g in range(group):
                value = source[x0 + g + a, pl.ds(0, (size_y + 2) * zc), :]
                value = value.reshape(pairs + 1, 2, zc, 128)
                halves[0].append(value[:, 0])
                halves[1].append(value[:, 1])
            parts.append(halves)
        for b in range(4):
            cut = [
                jnp.concatenate(
                    [
                        v[b // 2 : b // 2 + pairs].reshape(pairs * zc, 128)
                        for v in halves[b % 2]
                    ],
                    axis=0,
                ).astype(BF16)
                for halves in parts
            ]
            term = dot(jnp.concatenate(cut, axis=1), weight[4 * a + b])
            summed = term if summed is None else summed + term
    return summed


def coarse_conv(body, low, high, weight, zc):
    size_x, rows = body.shape[0] - 2, body.shape[1] - 2 * zc
    summed = None
    for a in range(3):
        for b in range(3):
            lhs = jnp.concatenate(
                [
                    jnp.concatenate(
                        [ref[x + a, pl.ds(b * zc, rows), :] for x in range(size_x)], axis=0
                    ).astype(BF16)
                    for ref in (low, body, high)
                ],
                axis=1,
            )
            tap = 9 * a + 3 * b
            kernel = jnp.concatenate([weight[tap], weight[tap + 1], weight[tap + 2]], axis=1)
            term = dot(lhs, kernel)
            summed = term if summed is None else summed + term
    return summed


def unet(
    sizes,
    cells_ref, lift_ref, encode_hbm, downward_hbm, first_hbm, second_hbm, up_hbm,
    decode_hbm, head_ref,
    out_ref,
    block, before, after, cell_first, cell_last, joint, lhs32, lhs16, chunks, fp, fe, sp, sf, se, up, ue, acc,
    s_below, s_above, s_first, s_last,
    coarse_bufs, middle_bufs, deep_bufs, low, middle, high,
    encode_raw, downward_raw, first_w, second_w, up_ref, decode_raw,
    encode_w, skip_w, wide_w,
    load_sems, send_sems, recv_sems,
):
    comps, size_x, size_y, size_z, rows_y = sizes
    zc, yc, xc = size_z // 2, size_y // 2, size_x // 2
    loads = [
        pltpu.make_async_copy(src, dst, load_sems.at[i])
        for i, (src, dst) in enumerate(
            (
                (encode_hbm, encode_raw), (downward_hbm, downward_raw), (first_hbm, first_w),
                (decode_hbm, decode_raw), (second_hbm, second_w), (up_hbm, up_ref),
            )
        )
    ]
    for load in loads:
        load.start()
    barrier = pltpu.get_barrier_semaphore()
    for direction in DIRS:
        pl.semaphore_signal(barrier, inc=1, device_id=neighbour(direction), device_id_type=MESH)
    width, edge = comps * size_z, 2 * comps
    own_rows = lax.broadcasted_iota(jnp.int32, (size_y, 128), 1)
    rims = [None, None]
    for x in range(size_x):
        value = cells_ref[x].astype(F32)
        block[x + 2, pl.ds(1, size_y // RIM)] = value.reshape(size_y // RIM, RIM, 128).astype(
            BF16
        )
        for side, start in enumerate((0, width - edge)):
            kept = jnp.where((own_rows >= start) & (own_rows < start + edge), value, 0.0)
            shift = (edge * x - start) % 128
            kept = pltpu.roll(kept, shift, 1) if shift else kept
            rims[side] = kept if rims[side] is None else rims[side] + kept
    cell_first[...] = rims[0].reshape(size_y // RIM, RIM, 128).astype(BF16)
    cell_last[...] = rims[1].reshape(size_y // RIM, RIM, 128).astype(BF16)
    pl.semaphore_wait(barrier, len(DIRS))
    cell_copies = send_cells(
        block, before, after, cell_first, cell_last, send_sems.at[4], recv_sems.at[4]
    )

    groups = []
    for g in range(5):
        total = None
        for tap in range(2 * g, min(2 * g + 2, 9)):
            for c in range(3):
                piece = lift_ref[3 * tap + c].astype(F32)
                blank = jnp.zeros((piece.shape[0], 128 - comps), F32)
                piece = jnp.concatenate([piece, blank], axis=1)
                shift = 64 * (tap % 2) + comps * c
                piece = pltpu.roll(piece, shift, 1) if shift else piece
                total = piece if total is None else total + piece
        groups.append(total)
    loads[0].wait()
    build_fine(encode_raw, encode_w, 0, encode_raw.shape[2])
    loads[1].wait()
    downward = [
        jnp.concatenate([downward_raw[4 * a + t] for t in range(4)], axis=1) for a in range(2)
    ]
    for copy in cell_copies:
        copy.wait_recv()

    all_rows = size_y + 2 * RIM
    lane = lax.broadcasted_iota(jnp.int32, (all_rows, 128), 1)

    def turned(value, shift):
        return pltpu.roll(value, shift % 128, 1) if shift % 128 else value

    for x in range(size_x + 4):
        near, place = (
            (0, size_x - 2 + x) if x < 2 else (1, x - 2) if x < size_x + 2
            else (2, x - size_x - 2)
        )
        own = turned(flat(block[x]), edge)
        before_x = turned(flat(before[near]), -edge * place)
        after_x = turned(flat(after[near]), width + edge - edge * place)
        joint[x] = jnp.where(
            lane < edge,
            before_x,
            jnp.where(lane < edge + width, own, jnp.where(lane < width + 2 * edge, after_x, 0.0)),
        )
    half = half_mask(rows_y)
    for x in range(size_x + 2):
        for g in range(5):
            parts = [
                joint[x + tap // 3, pl.ds(RIM - 2 + tap % 3, rows_y), :]
                for tap in range(2 * g, min(2 * g + 2, 9))
            ]
            other = pltpu.roll(parts[1], 64, 1) if len(parts) > 1 else jnp.zeros_like(parts[0])
            lhs32[pl.ds(x * rows_y, rows_y), 128 * g : 128 * g + 128] = jnp.where(
                half, parts[0], other
            )
    lhs16[...] = lhs32[...].astype(BF16)

    for p in range(zc + 1):
        z_lo, z_hi = (2 * p, 2 * p + 1) if p < zc else (size_z, -1)
        kernel = jnp.concatenate(
            [
                jnp.concatenate(
                    [pltpu.roll(v, comps * (z + 1), 1) if z + 1 else v for v in groups], axis=1
                )
                for z in (z_lo, z_hi)
            ],
            axis=0,
        ).astype(BF16)
        chunks[p] = rounded(dot(lhs16[...], kernel)).astype(F32)
    for x in range(size_x + 2):
        span = pl.ds(x * rows_y, rows_y)
        for p in range(zc):
            fp[x, pl.ds(p, rows_y, stride=zc), :] = chunks[p, span, :]
            fe[x, pl.ds(p, rows_y, stride=zc), :] = jnp.where(
                half, chunks[p + 1, span, :], chunks[zc if p == 0 else p - 1, span, :]
            )

    c_body, c_below, c_above, c_first, c_last = coarse_bufs
    m_body, m_below, m_above, m_first, m_last = middle_bufs
    d_body, d_below, d_above, d_first, d_last = deep_bufs

    @pl.loop(0, xc)
    def _(x):
        skip = rounded(fine_conv(fp, fe, encode_w, 2 * x, 2, size_y, zc))
        half_rows = yc * zc
        coarse = None
        for g in range(2):
            part = skip[g * half_rows : (g + 1) * half_rows]
            term = dot(part, downward[g])
            coarse = term if coarse is None else coarse + term
            wide = part.astype(F32)
            plane = jnp.stack(
                [wide[:, :128].reshape(yc, zc, 128), wide[:, 128:].reshape(yc, zc, 128)], axis=1
            ).reshape(size_y, zc, 128)
            sp[2 * x + g + 1, pl.ds(1, size_y)] = plane.astype(BF16)
            s_first[2 * x + g] = plane[:, 0:1, :]
            s_last[2 * x + g] = plane[:, zc - 1 : zc, :]
        coarse = rounded(coarse).astype(F32)
        c_body[x + 1, pl.ds(1, yc)] = coarse.reshape(yc, zc, 128).astype(BF16)
        c_first[x] = coarse.reshape(yc, zc, 128)[:, 0:1, :]
        c_last[x] = coarse.reshape(yc, zc, 128)[:, zc - 1 : zc, :]

    coarse_copies = exchange(*coarse_bufs, send_sems.at[0], recv_sems.at[0], zc)
    launch(coarse_copies)
    skip_copies = exchange(
        sp, s_below, s_above, s_first, s_last, send_sems.at[1], recv_sems.at[1], zc
    )

    launch([c for c, d in zip(skip_copies, DIRS) if d[0] == 0])

    def coarse_layer(bufs, weight, result):
        body, below, above = bufs[:3]
        for x in range(xc + 2):
            middle[x] = flat(body[x])
            down, upper = shifted(middle[x], spread(below[x], zc), spread(above[x], zc), zc)
            low[x] = down
            high[x] = upper
        value = rounded(coarse_conv(middle, low, high, weight, zc)).astype(F32)
        target, _, _, first, last = result
        for x in range(xc):
            part = value[x * yc * zc : (x + 1) * yc * zc]
            target[x + 1, pl.ds(1, yc)] = part.reshape(yc, zc, 128).astype(BF16)
            first[x] = part.reshape(yc, zc, 128)[:, 0:1, :]
            last[x] = part.reshape(yc, zc, 128)[:, zc - 1 : zc, :]

    loads[2].wait()
    loads[3].wait()
    channels = decode_raw.shape[2] // 2
    build_fine(decode_raw, skip_w, 0, channels)
    build_fine(decode_raw, wide_w, channels, 2 * channels)
    for copy in coarse_copies:
        copy.wait_recv()
    coarse_layer(coarse_bufs, first_w, middle_bufs)
    middle_copies = exchange(*middle_bufs, send_sems.at[2], recv_sems.at[2], zc)
    launch(middle_copies)
    launch([c for c, d in zip(skip_copies, DIRS) if d[0] != 0])

    for copy in middle_copies:
        copy.wait_recv()
    loads[4].wait()
    coarse_layer(middle_bufs, second_w, deep_bufs)
    deep_copies = exchange(*deep_bufs, send_sems.at[3], recv_sems.at[3], zc)
    launch(deep_copies)

    for copy in skip_copies:
        copy.wait_recv()
    fine_half = half_mask((size_y + 2) * zc)

    @pl.loop(0, size_x + 2)
    def _(x):
        sf[x] = flat(sp[x])
        down, upper = shifted(sf[x], spread(s_below[x], zc), spread(s_above[x], zc), zc)
        se[x] = jnp.where(fine_half, upper, down)

    loads[5].wait()

    @pl.loop(0, xc)
    def _(x):
        acc[x] = fine_conv(sf, se, skip_w, 2 * x, 2, size_y, zc)

    for copy in deep_copies:
        copy.wait_recv()
    coarse_rows = (yc + 2) * zc
    _, coarse_end = masks(coarse_rows, zc)

    def interleaved(value):
        even = value[:, 128:].reshape(yc + 2, zc, 128)[: yc + 1]
        odd = value[:, :128].reshape(yc + 2, zc, 128)[1:]
        return jnp.stack([even, odd], axis=1).reshape((size_y + 2) * zc, 128)

    for x in range(size_x + 2):
        source, a = (x + 1) // 2, (x + 1) % 2
        kernel = jnp.concatenate([up_ref[2 * a], up_ref[2 * a + 1]], axis=0)
        edge_rows = jnp.where(
            coarse_end, spread(d_above[source], zc), spread(d_below[source], zc)
        )
        plane = interleaved(rounded(dot(flat(d_body[source]).astype(BF16), kernel)).astype(F32))
        edge = interleaved(rounded(dot(edge_rows.astype(BF16), kernel)).astype(F32))
        down, upper = shifted(plane, edge, edge, zc)
        up[x] = plane
        ue[x] = jnp.where(fine_half, upper, down)

    @pl.loop(0, xc)
    def _(x):
        joined = rounded(acc[x] + fine_conv(up, ue, wide_w, 2 * x, 2, size_y, zc))
        result = dot(head_ref[...], joined)
        out_ref[2 * x] = result[:, : yc * zc]
        out_ref[2 * x + 1] = result[:, yc * zc :]

    for copy in cell_copies + coarse_copies + skip_copies + middle_copies + deep_copies:
        copy.wait_send()


def local(
    displacement, lift_weight, encode_weight, downward_weight, middle_first, middle_second,
    up_weight, decode_weight, head_weight,
):
    comps, size_x, size_y, size_z = displacement.shape
    c1, c2 = encode_weight.shape[1], middle_first.shape[1]
    xc, yc, zc = size_x // 2, size_y // 2, size_z // 2
    rows_y = size_y + 8

    cells = jnp.transpose(displacement, (1, 2, 3, 0)).reshape(size_x, size_y, -1)
    cells = jnp.pad(cells, ((0, 0), (0, 0), (0, 128 - cells.shape[-1])))
    up_w = up_weight.reshape(4, 2 * c1, c2)
    head = jnp.einsum("pq,ki->pkqi", jnp.eye(4, dtype=BF16), head_weight).reshape(
        4 * comps, 4 * c1
    )
    head = jnp.pad(head, ((0, 16 - 4 * comps), (0, 0)))

    def coarse_set():
        return [
            pltpu.VMEM((xc + 2, yc + 2, zc, 128), BF16),
            pltpu.VMEM((xc + 2, yc + 2, 1, 128), F32),
            pltpu.VMEM((xc + 2, yc + 2, 1, 128), F32),
            pltpu.VMEM((xc, yc, 1, 128), F32),
            pltpu.VMEM((xc, yc, 1, 128), F32),
        ]

    fine = pltpu.VMEM((size_x + 2, (size_y + 2) * zc, 128), F32)
    first = pltpu.VMEM((size_x + 2, rows_y * zc, 128), F32)
    vmem, anywhere = pl.BlockSpec(memory_space=pltpu.VMEM), pl.BlockSpec(memory_space=pltpu.HBM)
    result = pl.pallas_call(
        functools.partial(unet, (comps, size_x, size_y, size_z, rows_y)),
        out_shape=jax.ShapeDtypeStruct((size_x, 16, yc * zc), F32),
        in_specs=[vmem, vmem] + [anywhere] * 6 + [vmem],
        out_specs=vmem,
        scratch_shapes=[
            pltpu.VMEM((size_x + 4, size_y // RIM + 2, RIM, 128), BF16),
            pltpu.VMEM((3, size_y // RIM + 2, RIM, 128), BF16),
            pltpu.VMEM((3, size_y // RIM + 2, RIM, 128), BF16),
            pltpu.VMEM((size_y // RIM, RIM, 128), BF16),
            pltpu.VMEM((size_y // RIM, RIM, 128), BF16),
            pltpu.VMEM((size_x + 4, size_y + 2 * RIM, 128), F32),
            pltpu.VMEM(((size_x + 2) * rows_y, 640), F32),
            pltpu.VMEM(((size_x + 2) * rows_y, 640), BF16),
            pltpu.VMEM((zc + 1, (size_x + 2) * rows_y, 128), F32),
            first, first,
            pltpu.VMEM((size_x + 2, size_y + 2, zc, 128), BF16),
            fine, fine, fine, fine,
            pltpu.VMEM((xc, 2 * yc * zc, 4 * c1), F32),
            pltpu.VMEM((size_x + 2, size_y + 2, 1, 128), F32),
            pltpu.VMEM((size_x + 2, size_y + 2, 1, 128), F32),
            pltpu.VMEM((size_x, size_y, 1, 128), F32),
            pltpu.VMEM((size_x, size_y, 1, 128), F32),
            coarse_set(), coarse_set(), coarse_set(),
            pltpu.VMEM((xc + 2, (yc + 2) * zc, 128), F32),
            pltpu.VMEM((xc + 2, (yc + 2) * zc, 128), F32),
            pltpu.VMEM((xc + 2, (yc + 2) * zc, 128), F32),
            pltpu.VMEM(encode_weight.shape, BF16),
            pltpu.VMEM(downward_weight.shape, BF16),
            pltpu.VMEM(middle_first.shape, BF16),
            pltpu.VMEM(middle_second.shape, BF16),
            pltpu.VMEM(up_w.shape, BF16),
            pltpu.VMEM(decode_weight.shape, BF16),
            pltpu.VMEM((12, 4 * c1, 4 * c1), BF16),
            pltpu.VMEM((12, 4 * c1, 4 * c1), BF16),
            pltpu.VMEM((12, 4 * c1, 4 * c1), BF16),
            pltpu.SemaphoreType.DMA((6,)),
            pltpu.SemaphoreType.DMA((5, len(DIRS))),
            pltpu.SemaphoreType.DMA((5, len(DIRS))),
        ],
        compiler_params=pltpu.CompilerParams(
            collective_id=0, has_side_effects=True, vmem_limit_bytes=63 * 2**20
        ),
    )(
        cells, lift_weight, encode_weight, downward_weight, middle_first, middle_second, up_w,
        decode_weight, head,
    )
    head_out = result[:, : 4 * comps].reshape(size_x, 2, 2, comps, yc, zc)
    head_out = jnp.transpose(head_out, (3, 0, 4, 1, 5, 2)).reshape(displacement.shape)
    return displacement.astype(F32) + head_out


def solution(mesh):
    placed = (P(None, "gx", "gy", "gz"), P(), P(), P(), P(), P(), P(), P(), P())
    return jax.shard_map(
        local, mesh=mesh, in_specs=placed, out_specs=P(None, "gx", "gy", "gz"), check_vma=False
    )
```

profile of v0, /device:TPU:0, one launch (start us, length us, event | category | flops | bytes accessed | tf_op | source)
XLA Modules:
  0.0 44.0 jit_solution(6105326157567166758)
XLA Ops:
  0.0 0.0 copy-start
  0.0 0.8 %multiply_bitcast_fusion = bf16[4,3,4,64]{3,2,1,0:T(4,128)(2,1)S(1)} fusion(bf16[3,64]{1,0:T(4,128)(2,1)} %param.17, bf16[4,4]{1,0:T(4,128)(2,1)S(1)} %fusion), kind=kLoop, calls=%fused_computation.1 | loop fusion | flops 3072 | bytes 6560 | tf_op jit(solution)/shard_map/pq,ki->pkqi/transpose | solution.py:436
  0.8 0.1 reshape.17
  0.9 0.0 copy-start.1
  0.9 0.6 %pad.9.head_ref = bf16[16,256]{1,0:T(8,128)(2,1)} pad(bf16[12,256]{1,0:T(8,128)(2,1)S(1)} %reshape.17, bf16[]{:T(256)} %constant.2.clone.1), padding=0_4x0_0 | pad | bytes 14338 | tf_op jit(solution)/shard_map/jit(_pad)/pad | solution.py:439
  1.5 0.0 copy-done
  1.5 0.1 copy.23
  1.6 0.6 %pad.8.cells_ref = bf16[4,32,128]{2,1,0:T(8,128)(2,1)} pad(bf16[4,32,48]{2,1,0:T(8,128)(2,1)S(1)} %copy.23, bf16[]{:T(256)} %constant.2.clone.1), padding=0_0x0_0x0_80 | pad | bytes 45058 | tf_op jit(solution)/shard_map/jit(_pad)/pad | solution.py:434
  2.2 0.0 copy-done.1
  2.2 0.0 copy-start.2
  2.2 0.8 %copy.25.downward_hbm = bf16[8,128,64]{2,1,0:T(8,128)(2,1)} copy(bf16[8,128,64]{1,2,0:T(8,128)(2,1)S(1)} %copy-done.1) | data formatting | bytes 262144 | tf_op args[3]
  3.1 0.0 copy-done.2
  3.1 1.0 %copy.24.lift_ref = bf16[27,64,3]{2,1,0:T(8,128)(2,1)} copy(bf16[27,64,3]{1,0,2:T(8,128)(2,1)S(1)} %copy-done.2) | data formatting | bytes 20736 | tf_op args[1]
  4.1 36.5 %shard_map.91 = f32[4,16,128]{2,1,0:T(8,128)} custom-call(bf16[4,32,128]{2,1,0:T(8,128)(2,1)} %pad.8.cells_ref, bf16[27,64,3]{2,1,0:T(8,128)(2,1)} %copy.24.lift_ref, bf16[27,64,64]{2,1,0:T(8,128)(2,1)} %encode_hbm.1, bf16[8,128,64]{2,1,0:T(8,128)(2,1)} %copy.25.downward_hbm, bf16[27,128,128]{2,1,0:T(8,128)(2,1)} %first_hbm.1, ...), custom_call_target="tpu_custom_call" | custom-call | tf_op jit(solution)/shard_map/pallas_call | solution.py:453
  40.6 0.8 %copy.26 = f32[4,12,128]{2,0,1:T(4,128)S(1)} copy(f32[4,12,128]{2,1,0:T(8,128)} %bitcast.15) | data formatting | bytes 49152 | tf_op jit(solution)/shard_map/slice | solution.py:500
  41.4 0.2 reshape.18
  41.6 1.3 %copy.27 = f32[3,4,16,2,8,2]{1,5,4,3,2,0:T(2,128)S(1)} copy(f32[3,4,16,2,8,2]{4,2,1,0,5,3:T(8,128)S(1)} %bitcast.11) | data formatting | bytes 49152 | tf_op jit(solution)/shard_map/transpose | solution.py:501
  42.9 0.4 copy.28
  43.3 0.7 %convert_add_fusion = f32[3,4,32,16]{2,3,1,0:T(8,128)} fusion(f32[3,4,32,16]{2,3,1,0:T(8,128)S(1)} %copy.28, bf16[3,4,32,16]{2,3,1,0:T(8,128)(2,1)S(1)} %copy-done), kind=kLoop, calls=%fused_computation | loop fusion | flops 12288 | bytes 61440 | tf_op jit(solution)/shard_map/add | solution.py:502
  (2 shorter events, 0.0 us)
Async XLA Ops:
  0.0 1.5 %copy-start = (bf16[3,4,32,16]{2,3,1,0:T(8,128)(2,1)S(1)}, bf16[3,4,32,16]{2,3,1,0:T(8,128)(2,1)}, u32[]{:S(2)}) copy-start(bf16[3,4,32,16]{2,3,1,0:T(8,128)(2,1)} %param.9) | copy-start | bytes 36868
  0.9 1.4 %copy-start.1 = (bf16[8,128,64]{1,2,0:T(8,128)(2,1)S(1)}, bf16[8,128,64]{1,2,0:T(8,128)(2,1)}, u32[]{:S(2)}) copy-start(bf16[8,128,64]{1,2,0:T(8,128)(2,1)} %param.12) | copy-start | bytes 393220
  2.2 0.9 %copy-start.2 = (bf16[27,64,3]{1,0,2:T(8,128)(2,1)S(1)}, bf16[27,64,3]{1,0,2:T(8,128)(2,1)}, u32[]{:S(2)}) copy-start(bf16[27,64,3]{1,0,2:T(8,128)(2,1)} %param.10) | copy-start | bytes 31108
where the time goes:
time: 44.2 us; the launch traced here: 44 us
  Pallas kernels  36.5 us (83%)
  local copies, waits for them, and re-layouts  6.04 us (14%)
  other arithmetic  1.43 us (3%)
    pallas_call x1, Pallas kernels, local(): pl.pallas_call(functools.partial(unet, (comps, size_x, size_y, size_z, ro...  36.5 us
    unnamed x8, local copies, waits for them, and re-layouts  1.88 us
    transpose x1, local copies, waits for them, and re-layouts, local(): jnp.transpose(head_out, (3, 0, 4, 1, 5, 2)).reshape(displacement.shape)  1.31 us

commit v1 on v0

v1 whole, which is shorter than its diff:
```python
import functools

import jax
import jax.numpy as jnp
from jax import lax
from jax.experimental import pallas as pl
from jax.experimental.pallas import tpu as pltpu
from jax.sharding import PartitionSpec as P

MESH = pl.DeviceIdType.MESH
NT = (((1,), (1,)), ((), ()))
NN = (((1,), (0,)), ((), ()))
F32, BF16 = jnp.float32, jnp.bfloat16
TILE, LANES = 8, 128


def leaky(value):
    return jnp.maximum(value, 0.1 * value)


def rounded(value):
    return leaky(value).astype(BF16)


def dot(rows, weight):
    return lax.dot_general(rows, weight, NT, preferred_element_type=F32)


def build_fine(raw, wide, lo, hi):
    out = raw.shape[1]
    blank = jnp.zeros((2 * out, wide.shape[2]), BF16)
    zero = jnp.zeros((out, hi - lo), BF16)
    for a in range(3):
        wide[4 * a, 2 * out :, :] = blank
        wide[4 * a + 3, : 2 * out, :] = blank
        for b in range(3):
            taps = [raw[9 * a + 3 * b + c][:, lo:hi] for c in range(3)]
            low = jnp.concatenate([taps[1], taps[2], zero, taps[0]], axis=1)
            high = jnp.concatenate([taps[0], taps[1], taps[2], zero], axis=1)
            pair = jnp.concatenate([low, high], axis=0)
            wide[4 * a + b, : 2 * out, :] = pair
            wide[4 * a + b + 1, 2 * out :, :] = pair


def build_coarse(raw, wide):
    out = raw.shape[1]
    blank = jnp.zeros((out, raw.shape[2]), BF16)
    for a in range(3):
        for b in range(3):
            for offset in range(2):
                tile = 6 * a + 2 * b + offset
                for side in range(2):
                    for e in range(2):
                        c = 2 * offset + e - side
                        block = raw[9 * a + 3 * b + c] if 0 <= c <= 2 else blank
                        wide[tile, out * side : out * (side + 1), LANES * e : LANES * (e + 1)] = block


def unet(
    dims,
    cells_hbm, lift_hbm, encode_hbm, downward_hbm, first_hbm, second_hbm, up_hbm, decode_hbm,
    head_hbm,
    out_ref,
    cells, lift_raw, head_raw, pack, window, joint, near, spread, lift_f, lift_rows, lift_w, select_w, chunks,
    fine_in, skip_scr, skip_in, wide_in, coarse_in, middle_in, deep_scr, up_scr, mine, final,
    head_f, head_w,
    encode_raw, downward_w, first_raw, second_raw, up_w, decode_raw,
    encode_w, skip_w, wide_w, first_w, second_w,
    load_sems, send_sems, recv_sems, swap_sems,
):
    ring_x, ring_y, ring_z = dims
    comps, size_x, size_z, size_y = cells.shape
    around = ring_x == 2
    steps = (0,) if around else (-1, 0, 1)
    pairs = ring_x // 2
    gx, gy, gz = lax.axis_index("gx"), lax.axis_index("gy"), lax.axis_index("gz")
    mine_x, pair = lax.rem(gx, 2), lax.div(gx, 2)

    def device(step, flip, shift_y, shift_z):
        side = 1 - mine_x if flip else mine_x
        return (
            2 * lax.rem(pair + pairs + step, pairs) + side,
            lax.rem(gy + ring_y + shift_y, ring_y),
            lax.rem(gz + ring_z + shift_z, ring_z),
        )

    links = [
        (step, flip, beside, dz)
        for step in steps for flip in (0, 1) for beside in (0, 1) for dz in (-1, 0, 1)
        if (step, flip, beside, dz) != (0, 0, 0, 0)
    ]
    barrier = pltpu.get_barrier_semaphore()
    for step, flip, beside, dz in links:
        shift = 2 * mine_x - 1 if beside else 0
        pl.semaphore_signal(
            barrier, inc=1, device_id=device(step, flip, shift, -dz), device_id_type=MESH
        )
    loads = [
        pltpu.make_async_copy(src, dst, load_sems.at[i])
        for i, (src, dst) in enumerate(
            (
                (cells_hbm, cells), (lift_hbm, lift_raw), (encode_hbm, encode_raw),
                (downward_hbm, downward_w), (first_hbm, first_raw), (second_hbm, second_raw),
                (up_hbm, up_w), (decode_hbm, decode_raw), (head_hbm, head_raw),
            )
        )
    ]
    for load in loads:
        load.start()

    loads[0].wait()
    for c in range(comps):
        total = None
        for x in range(size_x):
            value = cells[c, x].astype(F32)
            value = jnp.concatenate(
                [value, jnp.zeros((size_z, LANES - size_y), F32)], axis=1
            )
            value = pltpu.roll(value, size_y * x, 1) if x else value
            total = value if total is None else total + value
        pack[c] = total.reshape(size_z // TILE, TILE, LANES).astype(BF16)
    own_slot = mine_x if around else mine_x + 2
    tiles = size_z // TILE
    window[own_slot, 1 - mine_x, :, pl.ds(1, tiles)] = pack[...]
    pl.semaphore_wait(barrier, len(links))
    copies = []
    for number, (step, flip, beside, dz) in enumerate(links):
        side = 1 - mine_x if flip else mine_x
        shift = 1 - 2 * side if beside else 0
        row_slot = side if beside else 1 - side
        slot = mine_x if around else mine_x + 2 * (step + 1)
        start, count, place = {0: (0, tiles, 1), 1: (tiles - 1, 1, 0), -1: (0, 1, tiles + 1)}[dz]
        copies.append(
            pltpu.make_async_remote_copy(
                src_ref=pack.at[:, pl.ds(start, count)],
                dst_ref=window.at[slot, row_slot, :, pl.ds(place, count)],
                send_sem=send_sems.at[number], recv_sem=recv_sems.at[number],
                device_id=device(-step, flip, shift, dz), device_id_type=MESH,
            )
        )
    for copy in copies:
        copy.start()

    loads[1].wait()
    quarters = (size_z + 2 * TILE) // TILE
    slot_lanes = LANES // quarters
    for c in range(comps):
        value = lift_raw[c].astype(F32)
        spread[c] = jnp.concatenate([value, value], axis=1)
    depth = lift_w.shape[0]
    lift_f[pl.ds(0, depth), :] = jnp.zeros((depth, LANES), F32)
    for t in range(9):
        for cz in range(3):
            for c in range(comps):
                lift_f[pl.ds(slot_lanes * t + comps * cz + c, 1), :] = spread[
                    c, pl.ds(3 * t + cz, 1), :
                ]
    base = lift_f[pl.ds(0, depth), :]
    low_half = lax.broadcasted_iota(jnp.int32, (depth, LANES), 1) < LANES // 2
    for k in range(TILE // 2):
        even = pltpu.roll(base, comps * 2 * k, 0) if k else base
        odd = pltpu.roll(base, comps * (2 * k + 1), 0)
        lift_w[:, LANES * k : LANES * (k + 1)] = jnp.where(low_half, even, odd).astype(BF16)

    rows_s, lanes_s = select_w.shape
    zw = size_z + 2 * TILE
    row = lax.broadcasted_iota(jnp.int32, (rows_s, LANES), 0)
    lane = lax.broadcasted_iota(jnp.int32, (rows_s, LANES), 1)
    place, inside = lax.div(lane, slot_lanes), lax.rem(lane, slot_lanes)
    level = lax.div(inside, comps)
    comp = inside - comps * level
    for k in range(quarters):
        source = lax.rem(place + quarters - k, quarters)
        target = comp * zw + TILE * source - 1 + level
        hit = (row == target) & (inside < comps * (TILE + 2))
        select_w[:, LANES * k : LANES * (k + 1)] = jnp.where(hit, 1.0, 0.0).astype(BF16)

    loads[2].wait()
    build_fine(encode_raw, encode_w, 0, encode_raw.shape[2])
    loads[4].wait()
    build_coarse(first_raw, first_w)
    loads[5].wait()
    build_coarse(second_raw, second_w)
    loads[7].wait()
    channels = decode_raw.shape[2] // 2
    build_fine(decode_raw, skip_w, 0, channels)
    build_fine(decode_raw, wide_w, channels, 2 * channels)
    loads[8].wait()
    head_f[...] = jnp.zeros(head_f.shape, F32)
    for p in range(2):
        for q in range(2):
            for c in range(comps):
                value = head_raw[pl.ds(c, 1), :].astype(F32)
                other = jnp.zeros_like(value)
                head_f[
                    pl.ds(LANES * p + size_z * c + q, 1), LANES * p : LANES * (p + 1)
                ] = jnp.concatenate([other, value] if q else [value, other], axis=1)
    head_w[...] = head_f[...].astype(BF16)
    loads[3].wait()
    loads[6].wait()

    for copy in copies:
        copy.wait_recv()

    slots = window.shape[0]
    turned = jnp.concatenate(
        [
            jnp.swapaxes(window[s, r].astype(F32).reshape(comps * zw, LANES), 0, 1)
            for s in range(slots) for r in range(2)
        ],
        axis=0,
    ).astype(BF16)
    grouped = lax.dot_general(turned, select_w[...], NN, preferred_element_type=F32)
    tiles_y = size_y // TILE
    for s in range(slots):
        for r in range(2):
            part = grouped[LANES * (2 * s + r) : LANES * (2 * s + r + 1)]
            for k in range(quarters):
                joint[k, pl.ds(size_x * s, size_x), pl.ds(tiles_y * r, tiles_y)] = part[
                    :, LANES * k : LANES * (k + 1)
                ].reshape(size_x, tiles_y, TILE, LANES)
    planes_d, rows_n = near.shape[1], near.shape[2]
    first_tile = tiles_y - 2 - (tiles_y // 2) * mine_x
    for k in range(quarters):
        for x in range(planes_d):
            near[k, x] = joint[k, x, pl.ds(first_tile, rows_n // TILE)].reshape(rows_n, LANES)

    planes_f, planes_s = fine_in.shape[1], skip_in.shape[1]
    planes_c, planes_m, planes_e = coarse_in.shape[1], middle_in.shape[1], deep_scr.shape[0]
    planes_u = wide_in.shape[1]

    def source(plane, tap, total, shift=0):
        if around:
            return lax.rem(plane + tap + total - 1, total)
        return plane + tap + shift

    half_y = rows_n // 3
    slot_of = lax.div(lax.broadcasted_iota(jnp.int32, (half_y, LANES), 1), slot_lanes)

    @pl.loop(0, planes_f)
    def _(x):
        for parity in range(2):
            for q in range(quarters):
                for g in range(3):
                    taps = list(range(quarters * g, min(quarters * (g + 1), 9)))
                    value = None
                    for j, t in enumerate(taps):
                        part = near[
                            (j - q) % quarters, source(x, t // 3, planes_d),
                            pl.ds(TILE - 1 + parity + t % 3, half_y, stride=2), :,
                        ]
                        value = part if value is None else jnp.where(slot_of < j, value, part)
                    lift_rows[
                        q, pl.ds(pl.multiple_of(2 * half_y * x + half_y * parity, half_y), half_y),
                        LANES * g : LANES * (g + 1),
                    ] = value.astype(BF16)

    for q in range(quarters):
        value = leaky(
            lax.dot_general(lift_rows[q], lift_w[...], NN, preferred_element_type=F32)
        ).astype(BF16).astype(F32)
        for r in range(quarters):
            chunks[quarters * q + r] = value[:, LANES * r : LANES * (r + 1)]

    zpairs = zw // 2
    half = lax.broadcasted_iota(jnp.int32, (2 * half_y, LANES), 1) < LANES // 2

    @pl.loop(0, planes_f)
    def _(x):
        span = pl.ds(pl.multiple_of(2 * half_y * x, 2 * half_y), 2 * half_y)
        for zp in range(1, zpairs - 1):
            plane = chunks[zp, span, :]
            twin = jnp.where(half, chunks[zp + 1, span, :], chunks[zp - 1, span, :])
            for number, value in enumerate((plane, twin)):
                even, odd = value[:half_y], value[half_y:]
                for b, part in enumerate(
                    (pltpu.roll(odd, 1, 0), even, odd, pltpu.roll(even, half_y - 1, 0))
                ):
                    fine_in[
                        b, x, half_y * (zp - 1) : half_y * zp,
                        LANES * number : LANES * (number + 1),
                    ] = part.astype(BF16)

    inner = zpairs - 2
    quarter = TILE // 2
    own = zpairs - TILE
    wide_half = lax.broadcasted_iota(jnp.int32, (own, TILE, LANES), 2) < LANES // 2

    def store_pairs(target, x, scr, first):
        for b in range(4):
            lanes = slice(LANES * ((b + 1) % 2), LANES * ((b + 1) % 2) + LANES)
            rows = pl.ds(quarter + (b - 1) // 2 if b % 2 == 0 else quarter + b // 2, TILE)
            plane, above, below = (
                scr[pl.ds(first + d, own), rows, lanes] for d in (0, 1, -1)
            )
            twin = jnp.where(wide_half, above, below)
            target[b, x] = jnp.concatenate(
                [plane.reshape(own * TILE, LANES), twin.reshape(own * TILE, LANES)], axis=1
            ).astype(BF16)

    def store_coarse(target, x, z, value):
        lanes = slice(LANES * (z % 2), LANES * (z % 2) + LANES)
        for b, part in enumerate((pltpu.roll(value, 1, 0), value, pltpu.roll(value, half_y - 1, 0))):
            target[b, x, z // 2, :, lanes] = part.astype(BF16)

    rows_e = inner * half_y

    @pl.loop(0, planes_c)
    def _(x):
        summed = None
        for a in range(3):
            for b in range(4):
                lhs = jnp.concatenate(
                    [fine_in[b, source(2 * x + g, a, planes_f)] for g in range(2)], axis=0
                )
                term = dot(lhs, encode_w[4 * a + b])
                summed = term if summed is None else summed + term
        skip = rounded(summed)
        coarse = None
        for g in range(2):
            part = skip[g * rows_e : (g + 1) * rows_e]
            term = lax.dot_general(part, downward_w[g], NN, preferred_element_type=F32)
            coarse = term if coarse is None else coarse + term
            skip_scr[g] = part.astype(F32).reshape(inner, half_y, 2 * LANES)
        coarse = rounded(coarse).astype(F32)
        for z in range(inner):
            store_coarse(coarse_in, x, z, coarse[half_y * z : half_y * (z + 1)])
        for g in range(2):
            store_pairs(skip_in, 2 * x + g, skip_scr.at[g], (inner - own) // 2)

    def coarse_conv(target, weight, planes, count):
        total = target.shape[1]
        summed = None
        for a in range(3):
            for b in range(3):
                for offset in range(2):
                    lhs = jnp.concatenate(
                        [
                            target[
                                b, (x + a - 1) % total if around else x + a,
                                offset : offset + count,
                            ].reshape(count * half_y, 2 * LANES)
                            for x in range(planes)
                        ],
                        axis=0,
                    )
                    term = dot(lhs, weight[6 * a + 2 * b + offset])
                    summed = term if summed is None else summed + term
        return rounded(summed)

    count = inner // 2 - 1
    middle = coarse_conv(coarse_in, first_w, planes_m, count).astype(F32)
    for x in range(planes_m):
        for z in range(2 * count):
            start = half_y * (count * x + z // 2)
            store_coarse(
                middle_in, x, z,
                middle[start : start + half_y, LANES * (z % 2) : LANES * (z % 2) + LANES],
            )
    count -= 1
    deep = coarse_conv(middle_in, second_w, planes_e, count)
    deep_scr[...] = deep.reshape(planes_e, count * half_y, 2 * LANES)

    @pl.loop(0, planes_e)
    def _(x):
        for a in range(2):
            for side in range(2):
                lhs = deep_scr[x, :, LANES * side : LANES * (side + 1)]
                value = rounded(dot(lhs, up_w[a])).astype(F32)
                for u in range(count):
                    up_scr[a, 2 * u + side] = value[half_y * u : half_y * (u + 1)]
        for a in range(2):
            store_pairs(wide_in, 2 * x + a, up_scr.at[a], count - own // 2)

    swap = None
    for turn in range(2):
        side = mine_x if turn else 1 - mine_x
        summed = None
        for array, weight, shift in ((skip_in, skip_w, 5), (wide_in, wide_w, 1)):
            total = array.shape[1]
            for a in range(3):
                for b in range(4):
                    lhs = jnp.concatenate(
                        [
                            array[b, source(size_x * side + g, a, total, shift)]
                            for g in range(size_x)
                        ],
                        axis=0,
                    )
                    term = dot(lhs, weight[4 * a + b])
                    summed = term if summed is None else summed + term
        result = dot(rounded(summed), head_w[...])
        for g in range(size_x):
            for p in range(2):
                total = None
                for z in range(own):
                    start = TILE * (own * g + z)
                    value = result[start : start + TILE, LANES * p : LANES * (p + 1)]
                    value = pltpu.roll(value, 2 * z, 1) if z else value
                    total = value if total is None else total + value
                if turn:
                    final[g, mine_x, pl.ds(p, TILE, stride=2), :] = total
                else:
                    mine[g, pl.ds(p, TILE, stride=2), :] = total
        if not turn:
            swap = pltpu.make_async_remote_copy(
                src_ref=mine, dst_ref=final.at[:, mine_x],
                send_sem=swap_sems.at[0], recv_sem=swap_sems.at[1],
                device_id=device(0, 1, 0, 0), device_id_type=MESH,
            )
            swap.start()
    swap.wait_recv()
    flat = jnp.swapaxes(final[...].reshape(LANES, LANES), 0, 1)
    for c in range(comps):
        block = flat[size_z * c : size_z * (c + 1)]
        for x in range(size_x):
            value = pltpu.roll(block, LANES - size_y * x, 1) if x else block
            out_ref[c, x] = cells[c, x].astype(F32) + value[:, :size_y]
    for copy in copies:
        copy.wait_send()
    swap.wait_send()


def local(
    rings, displacement, lift_weight, encode_weight, downward_weight, middle_first, middle_second,
    up_weight, decode_weight, head_weight,
):
    comps, size_x, size_y, size_z = displacement.shape
    c1, c2 = encode_weight.shape[1], middle_first.shape[1]
    around = rings[0] == 2
    slots = 2 if around else 6
    span = 2 * size_x
    halo = (lambda h: 0) if around else (lambda h: h)
    zw, yh = size_z + 2 * TILE, (size_y // 2 + 2 * TILE) // 2
    zpairs, quarters = zw // 2, zw // TILE
    planes_d, planes_f, planes_s = (span + 2 * halo(h) for h in (8, 7, 6))
    planes_c, planes_m, planes_e = (span // 2 + 2 * halo(h) for h in (3, 2, 1))
    depth = 3 * LANES

    cells = jnp.transpose(displacement, (0, 1, 3, 2))
    lift = jnp.transpose(lift_weight, (2, 0, 1))
    downward = jnp.transpose(downward_weight, (0, 2, 1)).reshape(2, 4 * c1, c2)
    up_w = up_weight.reshape(2, 4 * c1, c2)
    anywhere = pl.BlockSpec(memory_space=pltpu.HBM)
    links = (11 if around else 35)
    v = pltpu.VMEM
    result = pl.pallas_call(
        functools.partial(unet, rings),
        out_shape=jax.ShapeDtypeStruct(cells.shape, F32),
        in_specs=[anywhere] * 9,
        out_specs=pl.BlockSpec(memory_space=pltpu.VMEM),
        scratch_shapes=[
            v(cells.shape, BF16), v(lift.shape, BF16), v(head_weight.shape, BF16),
            v((comps, size_z // TILE, TILE, LANES), BF16),
            v((slots, 2, comps, quarters, TILE, LANES), BF16),
            v((quarters, size_x * slots, 2 * size_y // TILE, TILE, LANES), F32),
            v((quarters, planes_d, 3 * yh, LANES), F32),
            v((comps, lift.shape[1], LANES), F32), v((depth, LANES), F32),
            v((quarters, planes_f * 2 * yh, depth), BF16),
            v((depth, quarters * LANES), BF16),
            v((comps * zw, quarters * LANES), BF16),
            v((zpairs, planes_f * 2 * yh, LANES), F32),
            v((4, planes_f, (zpairs - 2) * yh, 2 * LANES), BF16),
            v((2, zpairs - 2, yh, 2 * LANES), F32),
            v((4, planes_s, (zpairs - TILE) * TILE, 2 * LANES), BF16),
            v((4, 2 * planes_e, (zpairs - TILE) * TILE, 2 * LANES), BF16),
            v((3, planes_c, zpairs // 2 - 1, yh, 2 * LANES), BF16),
            v((3, planes_m, zpairs // 2 - 2, yh, 2 * LANES), BF16),
            v((planes_e, (zpairs // 2 - 3) * yh, 2 * LANES), BF16),
            v((2, zpairs - 6, yh, 2 * LANES), F32),
            v((size_x, 2 * TILE, LANES), F32),
            v((size_x, 2, 2 * TILE, LANES), F32),
            v((2 * LANES, 2 * LANES), F32), v((2 * LANES, 2 * LANES), BF16),
            v(encode_weight.shape, BF16), v(downward.shape, BF16), v(middle_first.shape, BF16),
            v(middle_second.shape, BF16), v(up_w.shape, BF16), v(decode_weight.shape, BF16),
            v((12, 4 * c1, 4 * c1), BF16), v((12, 4 * c1, 4 * c1), BF16),
            v((12, 4 * c1, 4 * c1), BF16),
            v((18, 2 * c2, 2 * c2), BF16), v((18, 2 * c2, 2 * c2), BF16),
            pltpu.SemaphoreType.DMA((9,)),
            pltpu.SemaphoreType.DMA((links,)), pltpu.SemaphoreType.DMA((links,)),
            pltpu.SemaphoreType.DMA((2,)),
        ],
        compiler_params=pltpu.CompilerParams(
            collective_id=0, has_side_effects=True, vmem_limit_bytes=63 * 2**20
        ),
    )(
        cells, lift, encode_weight, downward, middle_first, middle_second, up_w, decode_weight,
        head_weight,
    )
    return jnp.transpose(result, (0, 1, 3, 2))


def solution(mesh):
    placed = (P(None, "gx", "gy", "gz"), P(), P(), P(), P(), P(), P(), P(), P())
    rings = tuple(mesh.shape[axis] for axis in ("gx", "gy", "gz"))
    return jax.shard_map(
        functools.partial(local, rings), mesh=mesh, in_specs=placed,
        out_specs=P(None, "gx", "gy", "gz"), check_vma=False,
    )
```

time: 44.2 us -> 28.6 us (0.65)
  Pallas kernels: 36.5 us -> 26.9 us
  local copies, waits for them, and re-layouts: 6.04 us -> 1.54 us
  other arithmetic: 1.43 us -> 0 us
    pallas_call x1, Pallas kernels: 36.5 us -> 26.9 us  [local(): pl.pallas_call(functools.partial(unet, rings), out_shape=jax.ShapeDtypeSt...]
    transpose x2 -> x0, local copies, waits for them, and re-layouts: 1.33 us -> none  [the longest x1 1.31 us: local(): jnp.transpose(head_out, (3, 0, 4, 1, 5, 2)).reshape(displacement.shape)]
    pad x2 -> x0, local copies, waits for them, and re-layouts: 1.23 us -> none  [the longest x1 0.63 us: local(): cells = jnp.pad(cells, ((0, 0), (0, 0), (0, 128 - cells.shape[-1])))]
    reshape x4 -> x0, local copies, waits for them, and re-layouts: 0.83 us -> none  [the longest x1 0.41 us: local(): jnp.transpose(head_out, (3, 0, 4, 1, 5, 2)).reshape(displacement.shape)]
    slice x1 -> x0, local copies, waits for them, and re-layouts: 0.77 us -> none  [local(): head_out = result[:, :4 * comps].reshape(size_x, 2, 2, comps, yc, zc)]
    transpose x1 -> x0, other arithmetic: 0.77 us -> none  [local(): jnp.einsum('pq,ki->pkqi', jnp.eye(4, dtype=BF16), head_weight)]
    add x1 -> x0, other arithmetic: 0.66 us -> none  [local(): return displacement.astype(F32) + head_out]
    unnamed x8 -> x1, local copies, waits for them, and re-layouts: 1.88 us -> 1.54 us
where the time goes in v1:
time: 28.6 us; the launch traced here: 28.4 us
  Pallas kernels  26.9 us (94%)
  local copies, waits for them, and re-layouts  1.54 us (5%)
    pallas_call x1, Pallas kernels, local(): pl.pallas_call(functools.partial(unet, rings), out_shape=jax.ShapeDtypeSt...  26.9 us
    unnamed x1, local copies, waits for them, and re-layouts  1.54 us

profile of v1, /device:TPU:0, one launch (start us, length us, event | category | flops | bytes accessed | tf_op | source)
XLA Modules:
  0.0 28.4 jit_solution(2640356764104840243)
XLA Ops:
  0.0 26.9 %shard_map.91 = f32[3,4,16,32]{3,2,1,0:T(8,128)} custom-call(bf16[3,4,16,32]{3,2,1,0:T(8,128)(2,1)} %bitcast.10, bf16[3,27,64]{2,1,0:T(8,128)(2,1)} %bitcast.11, bf16[27,64,64]{2,1,0:T(8,128)(2,1)} %encode_hbm.1, bf16[2,256,128]{2,1,0:T(8,128)(2,1)} %bitcast.8, bf16[27,128,128]{2,1,0:T(8,128)(2,1)} %first_hbm.1, bf16[27,128,128]{2,1,0:T(8,128)(2,1)} %second_hbm.1, ...), custom_call_target="tpu_custom_call" | custom-call | tf_op jit(solution)/shard_map/pallas_call | solution.py:447
  26.9 1.5 %copy.11 = f32[3,4,32,16]{2,3,1,0:T(8,128)} copy(f32[3,4,32,16]{2,3,1,0:T(8,128)} %bitcast.7) | data formatting | bytes 49152

commit v2 on v1

--- a/solution.py
+++ b/solution.py
@@ -61,9 +61,9 @@
     cells_hbm, lift_hbm, encode_hbm, downward_hbm, first_hbm, second_hbm, up_hbm, decode_hbm,
     head_hbm,
     out_ref,
-    cells, lift_raw, head_raw, pack, window, joint, near, spread, lift_f, lift_rows, lift_w, select_w, chunks,
-    fine_in, skip_scr, skip_in, wide_in, coarse_in, middle_in, deep_scr, up_scr, mine, final,
-    head_f, head_w,
+    cells, lift_raw, head_raw, pack, window, joint, near, spread, lift_f, lift_rows, lift_w, select_w,
+    fine_in, skip_scr, skip_in, wide_in, coarse_in, middle_in, deep_scr, mine, final,
+    head_f, head_w, unit,
     encode_raw, downward_w, first_raw, second_raw, up_w, decode_raw,
     encode_w, skip_w, wide_w, first_w, second_w,
     load_sems, send_sems, recv_sems, swap_sems,
@@ -196,6 +196,7 @@
                     pl.ds(LANES * p + size_z * c + q, 1), LANES * p : LANES * (p + 1)
                 ] = jnp.concatenate([other, value] if q else [value, other], axis=1)
     head_w[...] = head_f[...].astype(BF16)
+    unit[...] = jnp.ones(unit.shape, F32)
     loads[3].wait()
     loads[6].wait()
 
@@ -225,7 +226,7 @@
         for x in range(planes_d):
             near[k, x] = joint[k, x, pl.ds(first_tile, rows_n // TILE)].reshape(rows_n, LANES)
 
-    planes_f, planes_s = fine_in.shape[1], skip_in.shape[1]
+    planes_f = fine_in.shape[2]
     planes_c, planes_m, planes_e = coarse_in.shape[1], middle_in.shape[1], deep_scr.shape[0]
     planes_u = wide_in.shape[1]
 
@@ -255,47 +256,50 @@
                         LANES * g : LANES * (g + 1),
                     ] = value.astype(BF16)
 
+    zpairs = zw // 2
+    half = lax.broadcasted_iota(jnp.int32, (planes_f, half_y, LANES), 2) < LANES // 2
     for q in range(quarters):
         value = leaky(
             lax.dot_general(lift_rows[q], lift_w[...], NN, preferred_element_type=F32)
-        ).astype(BF16).astype(F32)
+        )
         for r in range(quarters):
-            chunks[quarters * q + r] = value[:, LANES * r : LANES * (r + 1)]
-
-    zpairs = zw // 2
-    half = lax.broadcasted_iota(jnp.int32, (2 * half_y, LANES), 1) < LANES // 2
-
-    @pl.loop(0, planes_f)
-    def _(x):
-        span = pl.ds(pl.multiple_of(2 * half_y * x, 2 * half_y), 2 * half_y)
-        for zp in range(1, zpairs - 1):
-            plane = chunks[zp, span, :]
-            twin = jnp.where(half, chunks[zp + 1, span, :], chunks[zp - 1, span, :])
-            for number, value in enumerate((plane, twin)):
-                even, odd = value[:half_y], value[half_y:]
+            zp = quarters * q + r
+            for x in range(planes_f):
+                even, odd = (
+                    value[
+                        half_y * (2 * x + parity) : half_y * (2 * x + parity + 1),
+                        LANES * r : LANES * (r + 1),
+                    ]
+                    for parity in range(2)
+                )
                 for b, part in enumerate(
                     (pltpu.roll(odd, 1, 0), even, odd, pltpu.roll(even, half_y - 1, 0))
                 ):
-                    fine_in[
-                        b, x, half_y * (zp - 1) : half_y * zp,
-                        LANES * number : LANES * (number + 1),
-                    ] = part.astype(BF16)
+                    fine_in[b, zp, x, :, :LANES] = part.astype(BF16)
+        for zp in range(max(quarters * q - 1, 1), quarters * q + quarters - 1):
+            for b in range(4):
+                fine_in[b, zp, :, :, LANES:] = jnp.where(
+                    half, fine_in[b, zp + 1, :, :, :LANES], fine_in[b, zp - 1, :, :, :LANES]
+                )
 
     inner = zpairs - 2
     quarter = TILE // 2
     own = zpairs - TILE
-    wide_half = lax.broadcasted_iota(jnp.int32, (own, TILE, LANES), 2) < LANES // 2
-
-    def store_pairs(target, x, scr, first):
+    low = lax.broadcasted_iota(jnp.int32, (own * TILE, LANES), 1) < LANES // 2
+
+    def store_pairs(target, x, levels):
         for b in range(4):
-            lanes = slice(LANES * ((b + 1) % 2), LANES * ((b + 1) % 2) + LANES)
-            rows = pl.ds(quarter + (b - 1) // 2 if b % 2 == 0 else quarter + b // 2, TILE)
+            shift = quarter + (-1, 0, 0, 1)[b]
+            start = LANES * ((b + 1) % 2)
+            parts = [
+                pltpu.roll(level[:, start : start + LANES], half_y - shift, 0)[:TILE]
+                for level in levels
+            ]
             plane, above, below = (
-                scr[pl.ds(first + d, own), rows, lanes] for d in (0, 1, -1)
+                jnp.concatenate(parts[d : d + own], axis=0) for d in (1, 2, 0)
             )
-            twin = jnp.where(wide_half, above, below)
             target[b, x] = jnp.concatenate(
-                [plane.reshape(own * TILE, LANES), twin.reshape(own * TILE, LANES)], axis=1
+                [plane, jnp.where(low, above, below)], axis=1
             ).astype(BF16)
 
     def store_coarse(target, x, z, value):
@@ -305,32 +309,55 @@
 
     rows_e = inner * half_y
 
-    @pl.loop(0, planes_c)
-    def _(x):
+    def encode(x):
         summed = None
         for a in range(3):
             for b in range(4):
                 lhs = jnp.concatenate(
-                    [fine_in[b, source(2 * x + g, a, planes_f)] for g in range(2)], axis=0
+                    [
+                        fine_in[b, pl.ds(1, inner), source(2 * x + g, a, planes_f)].reshape(
+                            rows_e, 2 * LANES
+                        )
+                        for g in range(2)
+                    ],
+                    axis=0,
                 )
                 term = dot(lhs, encode_w[4 * a + b])
                 summed = term if summed is None else summed + term
-        skip = rounded(summed)
+        skip_scr[...] = rounded(summed)
+
+    def encoded(x):
         coarse = None
         for g in range(2):
-            part = skip[g * rows_e : (g + 1) * rows_e]
+            part = skip_scr[g * rows_e : (g + 1) * rows_e]
             term = lax.dot_general(part, downward_w[g], NN, preferred_element_type=F32)
             coarse = term if coarse is None else coarse + term
-            skip_scr[g] = part.astype(F32).reshape(inner, half_y, 2 * LANES)
         coarse = rounded(coarse).astype(F32)
         for z in range(inner):
             store_coarse(coarse_in, x, z, coarse[half_y * z : half_y * (z + 1)])
+        skirt = (inner - own) // 2 - 1
         for g in range(2):
-            store_pairs(skip_in, 2 * x + g, skip_scr.at[g], (inner - own) // 2)
+            levels = [
+                skip_scr[pl.ds(g * rows_e + half_y * (skirt + z), half_y)].astype(F32)
+                for z in range(own + 2)
+            ]
+            store_pairs(skip_in, 2 * x + g, levels)
+
+    encode(0)
+
+    @pl.loop(1, planes_c)
+    def _(x):
+        encoded(x - 1)
+        encode(x)
+
+    encoded(planes_c - 1)
+
+    def joined(sums):
+        return sums[0] + sums[1] * unit[...]
 
     def coarse_conv(target, weight, planes, count):
         total = target.shape[1]
-        summed = None
+        sums = [None, None]
         for a in range(3):
             for b in range(3):
                 for offset in range(2):
@@ -345,8 +372,8 @@
                         axis=0,
                     )
                     term = dot(lhs, weight[6 * a + 2 * b + offset])
-                    summed = term if summed is None else summed + term
-        return rounded(summed)
+                    sums[offset] = term if sums[offset] is None else sums[offset] + term
+        return rounded(joined(sums))
 
     count = inner // 2 - 1
     middle = coarse_conv(coarse_in, first_w, planes_m, count).astype(F32)
@@ -361,21 +388,19 @@
     deep = coarse_conv(middle_in, second_w, planes_e, count)
     deep_scr[...] = deep.reshape(planes_e, count * half_y, 2 * LANES)
 
-    @pl.loop(0, planes_e)
-    def _(x):
+    for x in range(planes_e):
+        sides = [deep_scr[x, :, LANES * side : LANES * (side + 1)] for side in range(2)]
         for a in range(2):
-            for side in range(2):
-                lhs = deep_scr[x, :, LANES * side : LANES * (side + 1)]
-                value = rounded(dot(lhs, up_w[a])).astype(F32)
-                for u in range(count):
-                    up_scr[a, 2 * u + side] = value[half_y * u : half_y * (u + 1)]
-        for a in range(2):
-            store_pairs(wide_in, 2 * x + a, up_scr.at[a], count - own // 2)
+            values = [rounded(dot(lhs, up_w[a])).astype(F32) for lhs in sides]
+            levels = [
+                values[z % 2][half_y * (z // 2) : half_y * (z // 2 + 1)] for z in range(own + 2)
+            ]
+            store_pairs(wide_in, 2 * x + a, levels)
 
     swap = None
     for turn in range(2):
         side = mine_x if turn else 1 - mine_x
-        summed = None
+        sums = [None, None]
         for array, weight, shift in ((skip_in, skip_w, 5), (wide_in, wide_w, 1)):
             total = array.shape[1]
             for a in range(3):
@@ -388,8 +413,8 @@
                         axis=0,
                     )
                     term = dot(lhs, weight[4 * a + b])
-                    summed = term if summed is None else summed + term
-        result = dot(rounded(summed), head_w[...])
+                    sums[b % 2] = term if sums[b % 2] is None else sums[b % 2] + term
+        result = dot(rounded(joined(sums)), head_w[...])
         for g in range(size_x):
             for p in range(2):
                 total = None
@@ -446,7 +471,7 @@
     v = pltpu.VMEM
     result = pl.pallas_call(
         functools.partial(unet, rings),
-        out_shape=jax.ShapeDtypeStruct(cells.shape, F32),
+        out_shape=pltpu.VMEM(cells.shape, F32),
         in_specs=[anywhere] * 9,
         out_specs=pl.BlockSpec(memory_space=pltpu.VMEM),
         scratch_shapes=[
@@ -459,18 +484,16 @@
             v((quarters, planes_f * 2 * yh, depth), BF16),
             v((depth, quarters * LANES), BF16),
             v((comps * zw, quarters * LANES), BF16),
-            v((zpairs, planes_f * 2 * yh, LANES), F32),
-            v((4, planes_f, (zpairs - 2) * yh, 2 * LANES), BF16),
-            v((2, zpairs - 2, yh, 2 * LANES), F32),
+            v((4, zpairs, planes_f, yh, 2 * LANES), BF16),
+            v((2 * (zpairs - 2) * yh, 2 * LANES), BF16),
             v((4, planes_s, (zpairs - TILE) * TILE, 2 * LANES), BF16),
             v((4, 2 * planes_e, (zpairs - TILE) * TILE, 2 * LANES), BF16),
             v((3, planes_c, zpairs // 2 - 1, yh, 2 * LANES), BF16),
             v((3, planes_m, zpairs // 2 - 2, yh, 2 * LANES), BF16),
             v((planes_e, (zpairs // 2 - 3) * yh, 2 * LANES), BF16),
-            v((2, zpairs - 6, yh, 2 * LANES), F32),
             v((size_x, 2 * TILE, LANES), F32),
             v((size_x, 2, 2 * TILE, LANES), F32),
-            v((2 * LANES, 2 * LANES), F32), v((2 * LANES, 2 * LANES), BF16),
+            v((2 * LANES, 2 * LANES), F32), v((2 * LANES, 2 * LANES), BF16), v((1, 2 * LANES), F32),
             v(encode_weight.shape, BF16), v(downward.shape, BF16), v(middle_first.shape, BF16),
             v(middle_second.shape, BF16), v(up_w.shape, BF16), v(decode_weight.shape, BF16),
             v((12, 4 * c1, 4 * c1), BF16), v((12, 4 * c1, 4 * c1), BF16),

time: 28.6 us -> 22.8 us (0.80)
  Pallas kernels: 26.9 us -> 22 us
  local copies, waits for them, and re-layouts: 1.54 us -> 0.64 us
    pallas_call x1, Pallas kernels: 26.9 us -> 22 us  [local(): pl.pallas_call(functools.partial(unet, rings), out_shape=pltpu.VMEM(cells...]
    unnamed x1, local copies, waits for them, and re-layouts: 1.54 us -> 0.64 us
where the time goes in v2:
time: 22.8 us; the launch traced here: 22.7 us
  Pallas kernels  22 us (96%)
  local copies, waits for them, and re-layouts  0.64 us (3%)
    pallas_call x1, Pallas kernels, local(): pl.pallas_call(functools.partial(unet, rings), out_shape=pltpu.VMEM(cells...  22 us
    unnamed x1, local copies, waits for them, and re-layouts  0.64 us

profile of v2, /device:TPU:0, one launch (start us, length us, event | category | flops | bytes accessed | tf_op | source)
XLA Modules:
  0.0 22.7 jit_solution(15955267598688423827)
XLA Ops:
  0.0 22.0 %shard_map.91 = f32[3,4,16,32]{3,2,1,0:T(8,128)S(1)} custom-call(bf16[3,4,16,32]{3,2,1,0:T(8,128)(2,1)} %bitcast.10, bf16[3,27,64]{2,1,0:T(8,128)(2,1)} %bitcast.11, bf16[27,64,64]{2,1,0:T(8,128)(2,1)} %encode_hbm.1, bf16[2,256,128]{2,1,0:T(8,128)(2,1)} %bitcast.8, bf16[27,128,128]{2,1,0:T(8,128)(2,1)} %first_hbm.1, bf16[27,128,128]{2,1,0:T(8,128)(2,1)} %second_hbm.1, ...), custom_call_target="tpu_custom_call" | custom-call | tf_op jit(solution)/shard_map/pallas_call | solution.py:472
  22.0 0.6 %copy.11 = f32[3,4,32,16]{2,3,1,0:T(8,128)} copy(f32[3,4,32,16]{2,3,1,0:T(8,128)S(1)} %bitcast.7) | data formatting | bytes 49152

commit v3 on v2

--- a/solution.py
+++ b/solution.py
@@ -62,7 +62,7 @@
     head_hbm,
     out_ref,
     cells, lift_raw, head_raw, pack, window, joint, near, spread, lift_f, lift_rows, lift_w, select_w,
-    fine_in, skip_scr, skip_in, wide_in, coarse_in, middle_in, deep_scr, mine, final,
+    fine_in, skip_two, skip_in, wide_in, coarse_in, middle_in, deep_scr, mine, final, ahead,
     head_f, head_w, unit,
     encode_raw, downward_w, first_raw, second_raw, up_w, decode_raw,
     encode_w, skip_w, wide_w, first_w, second_w,
@@ -232,6 +232,8 @@
 
     def source(plane, tap, total, shift=0):
         if around:
+            if isinstance(plane, int):
+                return (plane + tap - 1) % total
             return lax.rem(plane + tap + total - 1, total)
         return plane + tap + shift
 
@@ -309,8 +311,12 @@
 
     rows_e = inner * half_y
 
+    def joined(sums):
+        return sums[0] + sums[1] * unit[...]
+
     def encode(x):
-        summed = None
+        skip_scr = skip_two.at[x % 2]
+        sums = [None, None]
         for a in range(3):
             for b in range(4):
                 lhs = jnp.concatenate(
@@ -323,10 +329,11 @@
                     axis=0,
                 )
                 term = dot(lhs, encode_w[4 * a + b])
-                summed = term if summed is None else summed + term
-        skip_scr[...] = rounded(summed)
+                sums[b % 2] = term if sums[b % 2] is None else sums[b % 2] + term
+        skip_scr[...] = rounded(joined(sums))
 
     def encoded(x):
+        skip_scr = skip_two.at[x % 2]
         coarse = None
         for g in range(2):
             part = skip_scr[g * rows_e : (g + 1) * rows_e]
@@ -335,6 +342,9 @@
         coarse = rounded(coarse).astype(F32)
         for z in range(inner):
             store_coarse(coarse_in, x, z, coarse[half_y * z : half_y * (z + 1)])
+
+    def kept(x):
+        skip_scr = skip_two.at[x % 2]
         skirt = (inner - own) // 2 - 1
         for g in range(2):
             levels = [
@@ -345,15 +355,12 @@
 
     encode(0)
 
-    @pl.loop(1, planes_c)
-    def _(x):
+    for x in range(1, planes_c):
+        encode(x)
         encoded(x - 1)
-        encode(x)
+        kept(x - 1)
 
     encoded(planes_c - 1)
-
-    def joined(sums):
-        return sums[0] + sums[1] * unit[...]
 
     def coarse_conv(target, weight, planes, count):
         total = target.shape[1]
@@ -373,10 +380,29 @@
                     )
                     term = dot(lhs, weight[6 * a + 2 * b + offset])
                     sums[offset] = term if sums[offset] is None else sums[offset] + term
-        return rounded(joined(sums))
-
+        return joined(sums)
+
+    def decode(array, weight, side, shift, taps):
+        sums = [None, None]
+        for number, (a, b) in enumerate(taps):
+            lhs = jnp.concatenate(
+                [
+                    array[b, source(size_x * side + g, a, array.shape[1], shift)]
+                    for g in range(size_x)
+                ],
+                axis=0,
+            )
+            term = dot(lhs, weight[4 * a + b])
+            n = number % 2
+            sums[n] = term if sums[n] is None else sums[n] + term
+        return joined(sums)
+
+    taps = [(a, b) for a in range(3) for b in range(4)]
     count = inner // 2 - 1
-    middle = coarse_conv(coarse_in, first_w, planes_m, count).astype(F32)
+    middle = coarse_conv(coarse_in, first_w, planes_m, count)
+    kept(planes_c - 1)
+    ahead[...] = decode(skip_in, skip_w, 1 - mine_x, 5, taps[:6])
+    middle = rounded(middle).astype(F32)
     for x in range(planes_m):
         for z in range(2 * count):
             start = half_y * (count * x + z // 2)
@@ -386,7 +412,8 @@
             )
     count -= 1
     deep = coarse_conv(middle_in, second_w, planes_e, count)
-    deep_scr[...] = deep.reshape(planes_e, count * half_y, 2 * LANES)
+    ahead[...] += decode(skip_in, skip_w, 1 - mine_x, 5, taps[6:])
+    deep_scr[...] = rounded(deep).reshape(planes_e, count * half_y, 2 * LANES)
 
     for x in range(planes_e):
         sides = [deep_scr[x, :, LANES * side : LANES * (side + 1)] for side in range(2)]
@@ -400,29 +427,22 @@
     swap = None
     for turn in range(2):
         side = mine_x if turn else 1 - mine_x
-        sums = [None, None]
-        for array, weight, shift in ((skip_in, skip_w, 5), (wide_in, wide_w, 1)):
-            total = array.shape[1]
-            for a in range(3):
-                for b in range(4):
-                    lhs = jnp.concatenate(
-                        [
-                            array[b, source(size_x * side + g, a, total, shift)]
-                            for g in range(size_x)
-                        ],
-                        axis=0,
-                    )
-                    term = dot(lhs, weight[4 * a + b])
-                    sums[b % 2] = term if sums[b % 2] is None else sums[b % 2] + term
-        result = dot(rounded(joined(sums)), head_w[...])
-        for g in range(size_x):
-            for p in range(2):
+        if turn:
+            ahead[...] = decode(skip_in, skip_w, side, 5, taps)
+        summed = ahead[...] + decode(wide_in, wide_w, side, 1, taps)
+        result = dot(rounded(summed), head_w[...])
+        for p in range(2):
+            totals = []
+            for g in range(size_x):
                 total = None
                 for z in range(own):
                     start = TILE * (own * g + z)
                     value = result[start : start + TILE, LANES * p : LANES * (p + 1)]
                     value = pltpu.roll(value, 2 * z, 1) if z else value
                     total = value if total is None else total + value
+                totals.append(total)
+            for g in range(size_x // 2):
+                total = totals[g] + pltpu.roll(totals[g + size_x // 2], LANES // 2, 1)
                 if turn:
                     final[g, mine_x, pl.ds(p, TILE, stride=2), :] = total
                 else:
@@ -435,12 +455,14 @@
             )
             swap.start()
     swap.wait_recv()
-    flat = jnp.swapaxes(final[...].reshape(LANES, LANES), 0, 1)
+    flat = jnp.swapaxes(final[...].reshape(LANES // 2, LANES), 0, 1)
     for c in range(comps):
-        block = flat[size_z * c : size_z * (c + 1)]
         for x in range(size_x):
-            value = pltpu.roll(block, LANES - size_y * x, 1) if x else block
-            out_ref[c, x] = cells[c, x].astype(F32) + value[:, :size_y]
+            start = LANES // 2 * (2 * x // size_x) + size_z * c
+            shift = size_y * (x % (size_x // 2))
+            out_ref[c, x] = cells[c, x].astype(F32) + flat[
+                start : start + size_z, shift : shift + size_y
+            ]
     for copy in copies:
         copy.wait_send()
     swap.wait_send()
@@ -485,14 +507,15 @@
             v((depth, quarters * LANES), BF16),
             v((comps * zw, quarters * LANES), BF16),
             v((4, zpairs, planes_f, yh, 2 * LANES), BF16),
-            v((2 * (zpairs - 2) * yh, 2 * LANES), BF16),
+            v((2, 2 * (zpairs - 2) * yh, 2 * LANES), BF16),
             v((4, planes_s, (zpairs - TILE) * TILE, 2 * LANES), BF16),
             v((4, 2 * planes_e, (zpairs - TILE) * TILE, 2 * LANES), BF16),
             v((3, planes_c, zpairs // 2 - 1, yh, 2 * LANES), BF16),
             v((3, planes_m, zpairs // 2 - 2, yh, 2 * LANES), BF16),
             v((planes_e, (zpairs // 2 - 3) * yh, 2 * LANES), BF16),
-            v((size_x, 2 * TILE, LANES), F32),
-            v((size_x, 2, 2 * TILE, LANES), F32),
+            v((size_x // 2, 2 * TILE, LANES), F32),
+            v((size_x // 2, 2, 2 * TILE, LANES), F32),
+            v((size_x * (zpairs - TILE) * TILE, 2 * LANES), F32),
             v((2 * LANES, 2 * LANES), F32), v((2 * LANES, 2 * LANES), BF16), v((1, 2 * LANES), F32),
             v(encode_weight.shape, BF16), v(downward.shape, BF16), v(middle_first.shape, BF16),
             v(middle_second.shape, BF16), v(up_w.shape, BF16), v(decode_weight.shape, BF16),

time: 22.8 us -> 21.7 us (0.952)
  Pallas kernels: 22 us -> 20.9 us
    pallas_call x1, Pallas kernels: 22 us -> 20.9 us  [local(): pl.pallas_call(functools.partial(unet, rings), out_shape=pltpu.VMEM(cells...]
where the time goes in v3:
time: 21.7 us; the launch traced here: 21.5 us
  Pallas kernels  20.9 us (96%)
  local copies, waits for them, and re-layouts  0.64 us (3%)
    pallas_call x1, Pallas kernels, local(): pl.pallas_call(functools.partial(unet, rings), out_shape=pltpu.VMEM(cells...  20.9 us
    unnamed x1, local copies, waits for them, and re-layouts  0.64 us

profile of v3, /device:TPU:0, one launch (start us, length us, event | category | flops | bytes accessed | tf_op | source)
XLA Modules:
  0.0 21.5 jit_solution(15462486626157918029)
XLA Ops:
  0.0 20.9 %shard_map.91 = f32[3,4,16,32]{3,2,1,0:T(8,128)S(1)} custom-call(bf16[3,4,16,32]{3,2,1,0:T(8,128)(2,1)} %bitcast.10, bf16[3,27,64]{2,1,0:T(8,128)(2,1)} %bitcast.11, bf16[27,64,64]{2,1,0:T(8,128)(2,1)} %encode_hbm.1, bf16[2,256,128]{2,1,0:T(8,128)(2,1)} %bitcast.8, bf16[27,128,128]{2,1,0:T(8,128)(2,1)} %first_hbm.1, bf16[27,128,128]{2,1,0:T(8,128)(2,1)} %second_hbm.1, ...), custom_call_target="tpu_custom_call" | custom-call | tf_op jit(solution)/shard_map/pallas_call | solution.py:494
  20.9 0.6 %copy.11 = f32[3,4,32,16]{2,3,1,0:T(8,128)} copy(f32[3,4,32,16]{2,3,1,0:T(8,128)S(1)} %bitcast.7) | data formatting | bytes 49152

commit v4 on v3

--- a/solution.py
+++ b/solution.py
@@ -26,7 +26,7 @@
     return lax.dot_general(rows, weight, NT, preferred_element_type=F32)
 
 
-def build_fine(raw, wide, lo, hi):
+def build_fine(raw, wide, lo, hi, odd=False):
     out = raw.shape[1]
     blank = jnp.zeros((2 * out, wide.shape[2]), BF16)
     zero = jnp.zeros((out, hi - lo), BF16)
@@ -35,8 +35,12 @@
         wide[4 * a + 3, : 2 * out, :] = blank
         for b in range(3):
             taps = [raw[9 * a + 3 * b + c][:, lo:hi] for c in range(3)]
-            low = jnp.concatenate([taps[1], taps[2], zero, taps[0]], axis=1)
-            high = jnp.concatenate([taps[0], taps[1], taps[2], zero], axis=1)
+            if odd:
+                low = jnp.concatenate([taps[0], taps[1], taps[2], zero], axis=1)
+                high = jnp.concatenate([zero, taps[0], taps[1], taps[2]], axis=1)
+            else:
+                low = jnp.concatenate([taps[1], taps[2], zero, taps[0]], axis=1)
+                high = jnp.concatenate([taps[0], taps[1], taps[2], zero], axis=1)
             pair = jnp.concatenate([low, high], axis=0)
             wide[4 * a + b, : 2 * out, :] = pair
             wide[4 * a + b + 1, 2 * out :, :] = pair
@@ -171,12 +175,12 @@
     comp = inside - comps * level
     for k in range(quarters):
         source = lax.rem(place + quarters - k, quarters)
-        target = comp * zw + TILE * source - 1 + level
+        target = comp * zw + TILE * source - 2 + level
         hit = (row == target) & (inside < comps * (TILE + 2))
         select_w[:, LANES * k : LANES * (k + 1)] = jnp.where(hit, 1.0, 0.0).astype(BF16)
 
     loads[2].wait()
-    build_fine(encode_raw, encode_w, 0, encode_raw.shape[2])
+    build_fine(encode_raw, encode_w, 0, encode_raw.shape[2], True)
     loads[4].wait()
     build_coarse(first_raw, first_w)
     loads[5].wait()
@@ -259,11 +263,15 @@
                     ] = value.astype(BF16)
 
     zpairs = zw // 2
-    half = lax.broadcasted_iota(jnp.int32, (planes_f, half_y, LANES), 2) < LANES // 2
-    for q in range(quarters):
-        value = leaky(
+    def lifted(q):
+        return leaky(
             lax.dot_general(lift_rows[q], lift_w[...], NN, preferred_element_type=F32)
         )
+
+    following = lifted(0)
+    for q in range(quarters):
+        value = following
+        following = lifted(q + 1) if q + 1 < quarters else None
         for r in range(quarters):
             zp = quarters * q + r
             for x in range(planes_f):
@@ -277,12 +285,7 @@
                 for b, part in enumerate(
                     (pltpu.roll(odd, 1, 0), even, odd, pltpu.roll(even, half_y - 1, 0))
                 ):
-                    fine_in[b, zp, x, :, :LANES] = part.astype(BF16)
-        for zp in range(max(quarters * q - 1, 1), quarters * q + quarters - 1):
-            for b in range(4):
-                fine_in[b, zp, :, :, LANES:] = jnp.where(
-                    half, fine_in[b, zp + 1, :, :, :LANES], fine_in[b, zp - 1, :, :, :LANES]
-                )
+                    fine_in[b, zp, x] = part.astype(BF16)
 
     inner = zpairs - 2
     quarter = TILE // 2
@@ -321,8 +324,14 @@
             for b in range(4):
                 lhs = jnp.concatenate(
                     [
-                        fine_in[b, pl.ds(1, inner), source(2 * x + g, a, planes_f)].reshape(
-                            rows_e, 2 * LANES
+                        jnp.concatenate(
+                            [
+                                fine_in[
+                                    b, pl.ds(d, inner), source(2 * x + g, a, planes_f)
+                                ].reshape(rows_e, LANES)
+                                for d in (1, 2)
+                            ],
+                            axis=1,
                         )
                         for g in range(2)
                     ],
@@ -506,7 +515,7 @@
             v((quarters, planes_f * 2 * yh, depth), BF16),
             v((depth, quarters * LANES), BF16),
             v((comps * zw, quarters * LANES), BF16),
-            v((4, zpairs, planes_f, yh, 2 * LANES), BF16),
+            v((4, zpairs, planes_f, yh, LANES), BF16),
             v((2, 2 * (zpairs - 2) * yh, 2 * LANES), BF16),
             v((4, planes_s, (zpairs - TILE) * TILE, 2 * LANES), BF16),
             v((4, 2 * planes_e, (zpairs - TILE) * TILE, 2 * LANES), BF16),

time: 21.7 us -> 21.4 us (0.986)
  Pallas kernels: 20.9 us -> 20.6 us
    pallas_call x1, Pallas kernels: 20.9 us -> 20.6 us  [local(): pl.pallas_call(functools.partial(unet, rings), out_shape=pltpu.VMEM(cells...]
where the time goes in v4:
time: 21.4 us; the launch traced here: 21.3 us
  Pallas kernels  20.6 us (96%)
  local copies, waits for them, and re-layouts  0.64 us (3%)
    pallas_call x1, Pallas kernels, local(): pl.pallas_call(functools.partial(unet, rings), out_shape=pltpu.VMEM(cells...  20.6 us
    unnamed x1, local copies, waits for them, and re-layouts  0.64 us

profile of v4, /device:TPU:0, one launch (start us, length us, event | category | flops | bytes accessed | tf_op | source)
XLA Modules:
  0.0 21.3 jit_solution(12591019644423128597)
XLA Ops:
  0.0 20.6 %shard_map.91 = f32[3,4,16,32]{3,2,1,0:T(8,128)S(1)} custom-call(bf16[3,4,16,32]{3,2,1,0:T(8,128)(2,1)} %bitcast.10, bf16[3,27,64]{2,1,0:T(8,128)(2,1)} %bitcast.11, bf16[27,64,64]{2,1,0:T(8,128)(2,1)} %encode_hbm.1, bf16[2,256,128]{2,1,0:T(8,128)(2,1)} %bitcast.8, bf16[27,128,128]{2,1,0:T(8,128)(2,1)} %first_hbm.1, bf16[27,128,128]{2,1,0:T(8,128)(2,1)} %second_hbm.1, ...), custom_call_target="tpu_custom_call" | custom-call | tf_op jit(solution)/shard_map/pallas_call | solution.py:503
  20.6 0.6 %copy.11 = f32[3,4,32,16]{2,3,1,0:T(8,128)} copy(f32[3,4,32,16]{2,3,1,0:T(8,128)S(1)} %bitcast.7) | data formatting | bytes 49152

commit v5 on v4

--- a/solution.py
+++ b/solution.py
@@ -244,10 +244,9 @@
     half_y = rows_n // 3
     slot_of = lax.div(lax.broadcasted_iota(jnp.int32, (half_y, LANES), 1), slot_lanes)
 
-    @pl.loop(0, planes_f)
-    def _(x):
-        for parity in range(2):
-            for q in range(quarters):
+    def rows_of(q):
+        for x in range(planes_f):
+            for parity in range(2):
                 for g in range(3):
                     taps = list(range(quarters * g, min(quarters * (g + 1), 9)))
                     value = None
@@ -258,12 +257,13 @@
                         ]
                         value = part if value is None else jnp.where(slot_of < j, value, part)
                     lift_rows[
-                        q, pl.ds(pl.multiple_of(2 * half_y * x + half_y * parity, half_y), half_y),
+                        q, pl.ds(half_y * (2 * x + parity), half_y),
                         LANES * g : LANES * (g + 1),
                     ] = value.astype(BF16)
 
     zpairs = zw // 2
     def lifted(q):
+        rows_of(q)
         return leaky(
             lax.dot_general(lift_rows[q], lift_w[...], NN, preferred_element_type=F32)
         )

time: 21.4 us -> 21.2 us (level)
  no operation moved by 1% of the time
where the time goes in v5:
time: 21.2 us; the launch traced here: 21.1 us
  Pallas kernels  20.4 us (96%)
  local copies, waits for them, and re-layouts  0.64 us (3%)
    pallas_call x1, Pallas kernels, local(): pl.pallas_call(functools.partial(unet, rings), out_shape=pltpu.VMEM(cells...  20.4 us
    unnamed x1, local copies, waits for them, and re-layouts  0.64 us

profile of v5, /device:TPU:0, one launch (start us, length us, event | category | flops | bytes accessed | tf_op | source)
XLA Modules:
  0.0 21.1 jit_solution(11046711785435434426)
XLA Ops:
  0.0 20.4 %shard_map.91 = f32[3,4,16,32]{3,2,1,0:T(8,128)S(1)} custom-call(bf16[3,4,16,32]{3,2,1,0:T(8,128)(2,1)} %bitcast.10, bf16[3,27,64]{2,1,0:T(8,128)(2,1)} %bitcast.11, bf16[27,64,64]{2,1,0:T(8,128)(2,1)} %encode_hbm.1, bf16[2,256,128]{2,1,0:T(8,128)(2,1)} %bitcast.8, bf16[27,128,128]{2,1,0:T(8,128)(2,1)} %first_hbm.1, bf16[27,128,128]{2,1,0:T(8,128)(2,1)} %second_hbm.1, ...), custom_call_target="tpu_custom_call" | custom-call | tf_op jit(solution)/shard_map/pallas_call | solution.py:503
  20.5 0.6 %copy.11 = f32[3,4,32,16]{2,3,1,0:T(8,128)} copy(f32[3,4,32,16]{2,3,1,0:T(8,128)S(1)} %bitcast.7) | data formatting | bytes 49152
